TPU v7x, 32 devices: a whole 2x2x4 slice. The times are simulated.
32 devices in a mesh: seq: 8 (over z, x), head: 4 (over y, core).
Axes of the slice: x: 2, y: 2, z: 4, core: 2. Of those that a mesh axis runs over, the one named last changes fastest.
Arguments:
- inputs: bfloat16 [2048, 3072], P('seq'), may hold values from -6 to 6
- decay_logs: float32 [12, 2048], P('head', 'seq'), may hold values from -3 to 0
- query_retain: bfloat16 [3072, 1536], P('seq', 'head'), may hold values from -0.109375 to 0.109375
- key_retain: bfloat16 [3072, 1536], P('seq', 'head'), may hold values from -0.109375 to 0.109375
- value_retain: bfloat16 [3072, 1536], P('seq', 'head'), may hold values from -0.109375 to 0.109375
- output_retain: bfloat16 [3072, 1536], P('seq', 'head'), may hold values from -0.15625 to 0.15625
- key_global: bfloat16 [3072, 512], P('seq', 'head')
- value_global: bfloat16 [3072, 512], P('seq', 'head'), may hold values from -0.109375 to 0.109375
- query_cross: bfloat16 [3072, 1536], P('seq', 'head')
Outputs:
- decoded: float32 [2048, 3072], P('seq')
- attended: bfloat16 [2048, 1536], P('seq', 'head')
All inputs are finite; a program needn't handle non-finite values.
Results may differ from a plain program's by a relative error of at most 0.028.
Values may be sent and summed in bfloat16 or wider, within the bound.
A program may use at most 192 MiB of HBM per device.

v0:
```python
from functools import partial

import jax
import jax.numpy as jnp
from jax import lax
from jax.sharding import PartitionSpec as P

HD = 128
KV_HEADS = 4
Q_CROSS = 12


def prefix_2(value, axis, join, neutral):
    count, mine = (lax.axis_size(axis), lax.axis_index(axis))
    pieces = jax.tree.map(lambda part: lax.all_gather(part, axis), value)
    total = jax.tree.map(
        lambda part, zero: jnp.full_like(part, 0) + jnp.asarray(zero, part.dtype), value, neutral
    )

    def turn(position, total):
        longer = join(total, jax.tree.map(lambda part: part[position], pieces))
        return jax.tree.map(lambda new, old: jnp.where(position < mine, new, old), longer, total)

    return lax.fori_loop(0, count - 1, turn, total)


def row_norm(values):
    return values * lax.rsqrt(jnp.mean(values * values, axis=-1, keepdims=True) + 1e-06)


def chain_join(earlier, later):
    return (earlier[0] * later[0], later[0][:, None, None] * earlier[1] + later[1])


def keep_state(carried_state):
    return carried_state


def attend_piece(query_set, query_positions, key_piece, value_piece, key_positions, carried_state):
    row_top, row_total, gathered_sum_total = carried_state
    scores = jnp.einsum("tgqd,sgd->gqts", query_set, key_piece, preferred_element_type=jnp.float32)
    allowed = key_positions[None, :] <= query_positions[:, None]
    masked = jnp.where(allowed, scores, -1e30)
    new_top = jnp.maximum(row_top, jnp.max(masked, axis=-1))
    weights = jnp.where(allowed, jnp.exp(masked - new_top[..., None]), 0.0)
    new_total = jnp.sum(weights, axis=-1)
    gathered = jnp.einsum(
        "gqts,sgd->gqtd",
        weights.astype(jnp.bfloat16),
        value_piece,
        preferred_element_type=jnp.float32,
    )
    return (new_top, new_total, gathered)


def finish_rows(carried_state):
    row_top, row_total, gathered_sum_total = carried_state
    result = gathered_sum_total / row_total[..., None]
    query_rows = result.shape[2]
    return result.transpose(2, 0, 1, 3).reshape(query_rows, -1).astype(jnp.bfloat16)


def body(
    inputs,
    decay_logs,
    query_retain,
    key_retain,
    value_retain,
    output_retain,
    key_global,
    value_global,
    query_cross,
):
    row_count = inputs.shape[0]
    inner_width = query_retain.shape[1]
    local_heads = inner_width // HD
    input_full = inputs.astype(jnp.float32)
    normed = row_norm(input_full).astype(jnp.bfloat16)
    pieces = (
        lax.all_gather(query_retain, "seq", axis=0, tiled=True),
        lax.all_gather(key_retain, "seq", axis=0, tiled=True),
        lax.all_gather(value_retain, "seq", axis=0, tiled=True),
    )
    queries, lookup_feature_width, value_columns = tuple(
        (
            jnp.dot(normed, weight_piece, preferred_element_type=jnp.float32)
            for weight_piece in pieces
        )
    )
    out_weights, key_weights, value_weights, cross_weights = (
        lax.all_gather(output_retain, "seq", axis=0, tiled=True),
        lax.all_gather(key_global, "seq", axis=0, tiled=True),
        lax.all_gather(value_global, "seq", axis=0, tiled=True),
        lax.all_gather(query_cross, "seq", axis=0, tiled=True),
    )

    def by_head(matrix):
        return matrix.astype(jnp.bfloat16).reshape(row_count, local_heads, HD).transpose(1, 0, 2)

    query_heads = by_head(queries)
    key_heads = by_head(lookup_feature_width)
    value_heads = by_head(value_columns)
    running = jnp.cumsum(decay_logs, axis=-1)
    causal = jnp.arange(row_count)[:, None] >= jnp.arange(row_count)[None, :]
    spread = jnp.where(causal[None], running[:, :, None] - running[:, None, :], 0.0)
    weights = jnp.where(causal[None], jnp.exp(spread), 0.0)
    scores = jnp.einsum("htd,hsd->hts", query_heads, key_heads, preferred_element_type=jnp.float32)
    weighted = (scores * weights).astype(jnp.bfloat16)
    tail_decay = jnp.exp(running[:, -1:] - running)
    faded_keys = (key_heads.astype(jnp.float32) * tail_decay[:, :, None]).astype(jnp.bfloat16)
    resident_state = jnp.einsum(
        "htd,hte->hde", faded_keys, value_heads, preferred_element_type=jnp.float32
    )
    block_decay = jnp.exp(running[:, -1])
    prefix = prefix_2(
        (block_decay, resident_state),
        "seq",
        chain_join,
        (jnp.ones_like(block_decay), jnp.zeros_like(resident_state)),
    )
    incoming = prefix[1]
    within_block = jnp.einsum(
        "hts,hse->hte", weighted, value_heads, preferred_element_type=jnp.float32
    )
    carried = (
        jnp.einsum(
            "htd,hde->hte",
            query_heads.astype(jnp.float32),
            incoming,
            precision=lax.Precision.HIGHEST,
        )
        * jnp.exp(running)[:, :, None]
    )
    retained = (
        row_norm(within_block + carried)
        .astype(jnp.bfloat16)
        .transpose(1, 0, 2)
        .reshape(row_count, inner_width)
    )
    partial_sum = lax.dot_general(
        retained, out_weights, (((1,), (1,)), ((), ())), preferred_element_type=jnp.float32
    )
    mixed = lax.psum(partial_sum.astype(jnp.bfloat16), "head").astype(jnp.float32)
    decoded = input_full + mixed
    normed_two = row_norm(decoded).astype(jnp.bfloat16)
    key_rows = jnp.dot(normed_two, key_weights, preferred_element_type=jnp.float32).astype(
        jnp.bfloat16
    )
    value_rows = jnp.dot(normed_two, value_weights, preferred_element_type=jnp.float32).astype(
        jnp.bfloat16
    )
    cross_rows = (
        jnp.dot(normed_two, cross_weights, preferred_element_type=jnp.float32) * HD ** (-0.5)
    ).astype(jnp.bfloat16)
    local_groups = key_rows.shape[1] // HD
    group_size = Q_CROSS // KV_HEADS
    seq_index = lax.axis_index("seq")
    row_numbers = jnp.arange(row_count, dtype=jnp.int32)
    query_positions = seq_index * row_count + row_numbers
    query_set = cross_rows.reshape(row_count, local_groups, group_size, HD)
    top_position = jnp.max(query_positions)
    start_state = (
        jnp.full((local_groups, group_size, row_count), -1e30, jnp.float32),
        jnp.zeros((local_groups, group_size, row_count), jnp.float32),
        jnp.zeros((local_groups, group_size, row_count, HD), jnp.float32),
    )
    pieces = (
        lax.all_gather(key_rows, "seq", axis=0, tiled=True),
        lax.all_gather(value_rows, "seq", axis=0, tiled=True),
    )
    piece_rows = pieces[0].shape[0]
    key_piece = pieces[0].reshape(piece_rows, local_groups, HD)
    value_piece = pieces[1].reshape(piece_rows, local_groups, HD)
    key_positions = jnp.arange(piece_rows, dtype=jnp.int32)
    needed = jnp.int32(0) <= top_position
    update = partial(
        attend_piece, query_set, query_positions, key_piece, value_piece, key_positions
    )
    final_state = lax.cond(needed, update, keep_state, start_state)
    attended = finish_rows(final_state)
    return (decoded, attended)


def solution(mesh):
    in_specs = (
        P("seq", None),
        P("head", "seq"),
        P("seq", "head"),
        P("seq", "head"),
        P("seq", "head"),
        P("seq", "head"),
        P("seq", "head"),
        P("seq", "head"),
        P("seq", "head"),
    )
    out_specs = (P("seq", None), P("seq", "head"))
    return jax.shard_map(body, mesh=mesh, in_specs=in_specs, out_specs=out_specs, check_vma=False)
```

profile of v0, /device:TPU:0, one launch (start us, length us, event | category | flops | bytes accessed | tf_op | source)
XLA Modules:
  0.0 423.6 jit_solution(4253401915456547216)
XLA Ops:
  10.1 0.9 reduce-window.6
  11.6 1.8 fusion.16
  13.5 51.2 %all-gather.11.cloned.1.call-done = bf16[3072,384]{1,0:T(8,128)(2,1)} async-done(((bf16[384,384]{1,0:T(8,128)(2,1)}), bf16[3072,384]{1,0:T(8,128)(2,1)}) %all-gather.11.cloned.1.call-update) | async-done | bytes 2359312 | tf_op jit(solution)/shard_map/all_gather | solution.py:81
  64.7 2.7 convolution_convert_fusion.2
  67.6 49.7 %all-gather.13.cloned.1.call-done = bf16[3072,384]{1,0:T(8,128)(2,1)} async-done(((bf16[384,384]{1,0:T(8,128)(2,1)}), bf16[3072,384]{1,0:T(8,128)(2,1)}) %all-gather.13.cloned.1.call-update) | async-done | bytes 2359312 | tf_op jit(solution)/shard_map/all_gather | solution.py:82
  117.3 2.7 convolution_convert_fusion.1
  120.1 0.9 fusion.32
  123.1 19.4 %all-reduce = f32[24]{0:T(128)S(1)} all-reduce(f32[24]{0:T(128)S(1)} %bitcast_dynamic-update-slice_fusion), channel_id=2, replica_groups=mesh['seq'=8,'head'=4] {'seq'}, use_global_device_ids=true, to_apply=%add | all-reduce | flops 24 | bytes 192
  142.6 27.3 %all-gather.9.cloned.1.call-done = bf16[3072,384]{1,0:T(8,128)(2,1)} async-done(((bf16[384,384]{1,0:T(8,128)(2,1)}), bf16[3072,384]{1,0:T(8,128)(2,1)}) %all-gather.9.cloned.1.call-update) | async-done | bytes 2359312 | tf_op jit(solution)/shard_map/all_gather | solution.py:80
  169.9 2.7 convolution_convert_fusion.3
  172.8 42.5 %all-gather.19.cloned.1.call-done = f32[24,128,128]{2,1,0:T(8,128)} async-done(((f32[3,128,128]{2,1,0:T(8,128)}), f32[24,128,128]{2,1,0:T(8,128)}) %all-gather.19.cloned.1.call-update) | async-done | bytes 1572880 | tf_op jit(solution)/shard_map/all_gather | solution.py:15
  215.3 7.4 %while.14 = (s32[]{:T(128)}, f32[3,128,128]{2,1,0:T(8,128)S(1)}, s32[]{:T(128)}, f32[8,3]{1,0:T(8,128)S(1)}, f32[8,3,128,128]{3,2,1,0:T(8,128)}, /*index=5*/s32[]{:T(128)}, s32[]{:T(128)}) while((s32[]{:T(128)}, f32[3,128,128]{2,1,0:T(8,128)S(1)}, s32[]{:T(128)}, f32[8,3]{1,0:T(8,128)S(1)}, f32[8,3,128,128]{3,2,1,0:T(8,128)}, ...), condition=%wide.region_4.5_spmd.clone, body=%wide.region_3.4_spmd.clone.sunk | while | flops 196612 | bytes 589965 | solution.py:24
  215.3 1.0 fusion.61
  216.3 1.0 fusion.61
  217.4 1.0 fusion.61
  218.5 1.0 fusion.61
  219.5 1.0 fusion.61
  220.6 1.0 fusion.61
  221.7 1.0 fusion.61
  223.7 43.9 %all-gather.15.cloned.1.call-done = bf16[3072,384]{1,0:T(8,128)(2,1)} async-done(((bf16[384,384]{1,0:T(8,128)(2,1)}), bf16[3072,384]{1,0:T(8,128)(2,1)}) %all-gather.15.cloned.1.call-update) | async-done | bytes 2359312 | tf_op jit(solution)/shard_map/all_gather | solution.py:91
  267.6 3.9 convolution_convert_fusion
  273.5 32.1 %all_gather.45 = bf16[3072,128]{1,0:T(8,128)(2,1)S(1)} all-gather(bf16[384,128]{1,0:T(8,128)(2,1)S(1)} %copy-done.2), channel_id=1, replica_groups=mesh['seq'=8,'head'=4] {'seq'}, dimensions={0}, use_global_device_ids=true | all-gather | bytes 884736 | tf_op jit(solution)/shard_map/all_gather | solution.py:92
  305.7 33.3 %all_gather.47 = bf16[3072,128]{1,0:T(8,128)(2,1)S(1)} all-gather(bf16[384,128]{1,0:T(8,128)(2,1)S(1)} %copy-done.3), channel_id=1, replica_groups=mesh['seq'=8,'head'=4] {'seq'}, dimensions={0}, use_global_device_ids=true | all-gather | bytes 884736 | tf_op jit(solution)/shard_map/all_gather | solution.py:93
  339.0 2.0 multiply_reduce_fusion
  341.3 1.3 copy-done
  343.2 33.4 %all_gather.46 = bf16[2048,128]{1,0:T(8,128)(2,1)S(1)} all-gather(bf16[256,128]{1,0:T(8,128)(2,1)S(1)} %convolution_convert_fusion.5), channel_id=1, replica_groups=mesh['seq'=8,'head'=4] {'seq'}, dimensions={0}, use_global_device_ids=true | all-gather | bytes 589824 | tf_op jit(solution)/shard_map/all_gather | solution.py:168
  377.2 31.2 %all_gather.48 = bf16[2048,128]{1,0:T(8,128)(2,1)S(1)} all-gather(bf16[256,128]{1,0:T(8,128)(2,1)S(1)} %convolution_convert_fusion.4), channel_id=1, replica_groups=mesh['seq'=8,'head'=4] {'seq'}, dimensions={0}, use_global_device_ids=true | all-gather | bytes 589824 | tf_op jit(solution)/shard_map/all_gather | solution.py:169
  408.4 2.6 fusion.20
  411.1 4.9 %conditional.1 = (f32[1,3,256]{2,1,0:T(4,128)S(1)}, f32[1,3,256,128]{2,3,1,0:T(8,128)S(1)}) conditional(s32[]{:T(128)} %convert_element_type.73, () %tuple.31, (s32[2048]{0:T(1024)S(1)}, s32[256]{0:T(256)S(1)}, bf16[256,384]{1,0:T(8,128)(2,1)S(1)}, bf16[2048,128]{1,0:T(8,128)(2,1)S(1)}, bf16[2048,128]{1,0:T(8,128)(2,1)S(1)}) %tuple.32), branch_computations={%region_9.10_spmd, %region_10.13_spmd} | conditional | flops 821558528 | bytes 23030800 | solution.py:179
  411.9 1.1 fusion
  413.0 1.5 fusion.7
  414.6 1.4 fusion.2
  (69 shorter events, 10.8 us)
Async XLA Ops:
  7.2 57.6 %copy-start.1 = (bf16[256,3072]{1,0:T(8,128)(2,1)S(1)}, bf16[256,3072]{1,0:T(8,128)(2,1)}, u32[]{:S(2)}) copy-start(bf16[256,3072]{1,0:T(8,128)(2,1)} %param.13) | copy-start | bytes 4718596
  7.2 57.6 %all-gather.11.cloned.1.call-start = ((), (), s32[]{:S(2)}) async-start(), calls=%async_computation.1 | async-start | bytes 2654208 | tf_op jit(solution)/shard_map/all_gather | solution.py:81
  7.9 109.4 %all-gather.13.cloned.1.call-start = ((), (), s32[]{:S(2)}) async-start(), calls=%async_computation.2 | async-start | bytes 2654208 | tf_op jit(solution)/shard_map/all_gather | solution.py:82
  8.7 161.3 %all-gather.9.cloned.1.call-start = ((), (), s32[]{:S(2)}) async-start(), calls=%async_computation | async-start | bytes 2654208 | tf_op jit(solution)/shard_map/all_gather | solution.py:80
  9.4 205.9 %all-gather.19.cloned.1.call-start = ((), (), s32[]{:S(2)}) async-start(), calls=%async_computation.6 | async-start | bytes 1769472 | tf_op jit(solution)/shard_map/all_gather | solution.py:15
  67.6 54.1 %copy-start.4 = (u32[32]{0:T(128)S(1)}, u32[32]{0:T(128)}, u32[]{:S(2)}) copy-start(u32[32]{0:T(128)} %constant.65) | copy-start | bytes 388
  121.1 146.5 %all-gather.15.cloned.1.call-start = ((), (), s32[]{:S(2)}) async-start(), calls=%async_computation.3 | async-start | bytes 2654208 | tf_op jit(solution)/shard_map/all_gather | solution.py:91
  121.7 217.3 %all-reduce.3.cloned.1.call-start = ((), (), s32[]{:S(2)}) async-start(), calls=%async_computation.4 | async-start | bytes 3145728 | tf_op jit(solution)/shard_map/psum | solution.py:143
  267.6 6.0 %copy-start.2 = (bf16[384,128]{1,0:T(8,128)(2,1)S(1)}, bf16[384,128]{1,0:T(8,128)(2,1)}, u32[]{:S(2)}) copy-start(bf16[384,128]{1,0:T(8,128)(2,1)} %param.19) | copy-start | bytes 294916
  271.4 34.2 %copy-start.3 = (bf16[384,128]{1,0:T(8,128)(2,1)S(1)}, bf16[384,128]{1,0:T(8,128)(2,1)}, u32[]{:S(2)}) copy-start(bf16[384,128]{1,0:T(8,128)(2,1)} %param.20) | copy-start | bytes 294916
  271.5 136.9 %all-gather.17.cloned.1.call-start = ((), (), s32[]{:S(2)}) async-start(), calls=%async_computation.5 | async-start | bytes 2654208 | tf_op jit(solution)/shard_map/all_gather | solution.py:94
  341.0 1.7 copy-start
Sparse Core Ops, SparseCore 0:
  10.2 54.5 all-gather.10
  66.9 50.3 all-gather.12
  119.5 50.3 all-gather.8
  172.5 42.6 all-gather.18
  217.3 50.2 all-gather.14
  271.6 41.3 all-reduce.2
  315.2 59.7 all-gather.16
where the time goes:
time: 424 us
  waiting for transfers between devices  218 us (51%)
  blocking collectives  150 us (35%)
  matrix products  20.1 us (5%)
  between operations  15.6 us (4%)
  other arithmetic  15 us (4%)
  local copies, waits for them, and re-layouts  4.69 us (1%)
    all_gather x1, waiting for transfers between devices, body(): lax.all_gather(key_retain, 'seq', axis=0, tiled=True)  51.2 us
    all_gather x1, waiting for transfers between devices, body(): lax.all_gather(value_retain, 'seq', axis=0, tiled=True)  49.7 us
    all_gather x1, waiting for transfers between devices, body(): lax.all_gather(output_retain, 'seq', axis=0, tiled=True)  43.9 us
    all_gather x1, waiting for transfers between devices, prefix_2(): pieces = jax.tree.map(lambda part: lax.all_gather(part, axis), value)  42.5 us
    all_gather x1, blocking collectives, body(): lax.all_gather(key_rows, 'seq', axis=0, tiled=True)  33.4 us
    all_gather x1, blocking collectives, body(): lax.all_gather(value_global, 'seq', axis=0, tiled=True)  33.3 us
    all_gather x1, blocking collectives, body(): lax.all_gather(key_global, 'seq', axis=0, tiled=True)  32.1 us
    all_gather x1, blocking collectives, body(): lax.all_gather(value_rows, 'seq', axis=0, tiled=True)  31.2 us
  transfers between devices with their start and end apart: 7, of which 5 were waited for; matrix products, arithmetic and copies ran while one was open for 6% of the time, Pallas kernels for 0%

commit v1 on v0

v1 whole, which is shorter than its diff:
```python
import functools

import jax
import jax.numpy as jnp
from jax import lax
from jax.experimental import pallas as pl
from jax.experimental.pallas import tpu as pltpu
from jax.sharding import PartitionSpec as P

HD = 128
F32 = jnp.float32
BF16 = jnp.bfloat16
MESH = pl.DeviceIdType.MESH
KEY, VALUE, QUERY, OUT, CROSS = range(5)


def dot(a, b, dims=((1,), (0,)), precision=None):
    return lax.dot_general(a, b, (dims, ((), ())), precision=precision, preferred_element_type=F32)


def kernel(
    n,
    x_ref, run_row_ref, run_col_ref, tot_ref,
    wk_ref, wv_ref, wq_ref, wo_ref, wc_ref,
    dec_ref, att_ref,
    gk, gv, gq, go, gc, tots, states, kvs,
    normed, q_buf, k_buf, v_buf, ret, part, got_a, pair, got_b, mine, got_c,
    q_rows, top, total, acc,
    w_send, w_recv, wx_send, w_local, t_send, t_recv,
    s_send, s_recv, sx_send, kv_send, kv_recv, kvx_send, h_send, h_recv,
):
    me = lax.axis_index("seq")
    head = lax.axis_index("head")
    rows, width = x_ref.shape
    heads = wq_ref.shape[1] // HD
    half_n = n // 2
    twin = me + 1 - 2 * lax.rem(me, 2)
    core = lax.rem(head, 2)
    near = head + 1 - 2 * core
    far = lax.rem(head + 2, 4)
    own_refs = (wk_ref, wv_ref, wq_ref, wo_ref, wc_ref)
    full_refs = (gk, gv, gq, go, gc)

    def peer(k):
        return lax.rem(me + 2 * k, n)

    def twin_peer(k):
        return lax.rem(twin + 2 * k, n)

    barrier = pltpu.get_barrier_semaphore()

    @pl.loop(0, n - 1)
    def _(k):
        pl.semaphore_signal(
            barrier, inc=1, device_id={"seq": lax.rem(me + 1 + k, n)}, device_id_type=MESH
        )

    for other in (near, far):
        pl.semaphore_signal(barrier, inc=1, device_id={"head": other}, device_id_type=MESH)
    pl.semaphore_wait(barrier, n + 1)

    def slot(m, o):
        depth = own_refs[m].shape[0]
        return full_refs[m].at[pl.ds(pl.multiple_of(o * depth, depth), depth), :]

    def z_copy(m, k):
        return pltpu.make_async_remote_copy(
            own_refs[m], slot(m, me), w_send.at[m, k], w_recv.at[m, me],
            device_id={"seq": peer(k)}, device_id_type=MESH)

    def own_to_twin(m):
        return pltpu.make_async_remote_copy(
            own_refs[m], slot(m, me), wx_send.at[m, 0], w_recv.at[m, me],
            device_id={"seq": twin}, device_id_type=MESH)

    def x_copy(m, k):
        o = peer(k)
        return pltpu.make_async_remote_copy(
            slot(m, o), slot(m, o), wx_send.at[m, k], w_recv.at[m, o],
            device_id={"seq": twin}, device_id_type=MESH)

    def w_arrival(m, o):
        return pltpu.make_async_remote_copy(
            slot(m, o), slot(m, o), wx_send.at[m, 0], w_recv.at[m, o],
            device_id={"seq": twin}, device_id_type=MESH)

    def local_copy(m):
        return pltpu.make_async_copy(own_refs[m], slot(m, me), w_local.at[m])

    def start_gather(m):
        own_to_twin(m).start()

        @pl.loop(1, half_n)
        def _(k):
            z_copy(m, k).start()

        local_copy(m).start()

    def forward(m):
        @pl.loop(1, half_n)
        def _(k):
            w_arrival(m, peer(k)).wait_recv()
            x_copy(m, k).start()

    def finish(m):
        @pl.loop(0, half_n)
        def _(k):
            w_arrival(m, twin_peer(k)).wait_recv()

        local_copy(m).wait()

    def finish_sends(m):
        own_to_twin(m).wait_send()

        @pl.loop(1, half_n)
        def _(k):
            z_copy(m, k).wait_send()
            x_copy(m, k).wait_send()

    def causal_ops(buf, send, recv, x_send):
        def direct(k):
            return pltpu.make_async_remote_copy(
                buf.at[me], buf.at[me], send.at[k], recv.at[me],
                device_id={"seq": me + 2 * k}, device_id_type=MESH)

        def across(o, k):
            return pltpu.make_async_remote_copy(
                buf.at[o], buf.at[o], x_send.at[k], recv.at[o],
                device_id={"seq": twin}, device_id_type=MESH)

        z = me // 2
        odd = lax.rem(me, 2)

        def start():
            @pl.when(odd == 0)
            def _():
                across(me, 0).start()

            @pl.loop(1, half_n - z)
            def _(k):
                direct(k).start()

        def relay():
            @pl.loop(1, z + 1)
            def _(k):
                o = me - 2 * k
                across(o, k).wait_recv()
                across(o, k).start()

        def finish():
            @pl.loop(0, z + odd)
            def _(k):
                across(me - 1 - 2 * k, 0).wait_recv()

        def finish_sends():
            @pl.when(odd == 0)
            def _():
                across(me, 0).wait_send()

            @pl.loop(1, half_n - z)
            def _(k):
                direct(k).wait_send()

            @pl.loop(1, z + 1)
            def _(k):
                across(me - 2 * k, k).wait_send()

        return start, relay, finish, finish_sends

    def total_copy(p):
        return pltpu.make_async_remote_copy(
            tot_ref, tots.at[me], t_send.at[p], t_recv.at[me],
            device_id={"seq": p}, device_id_type=MESH)

    @pl.loop(me + 1, n)
    def _(p):
        total_copy(p).start()

    start_gather(KEY)
    start_gather(VALUE)
    start_gather(QUERY)

    @pl.loop(0, rows // 32)
    def _(i):
        part_rows = pl.ds(i * 32, 32)
        x = x_ref[part_rows, :].astype(F32)
        normed[part_rows, :] = (
            x * lax.rsqrt(jnp.mean(x * x, axis=-1, keepdims=True) + 1e-06)).astype(BF16)

    forward(KEY)
    forward(VALUE)
    finish(KEY)
    k_buf[...] = dot(normed[...], gk[...]).astype(BF16)
    finish(VALUE)
    v_buf[...] = dot(normed[...], gv[...]).astype(BF16)
    for h in range(heads):
        cols = slice(h * HD, (h + 1) * HD)
        col = run_col_ref[:, h:h + 1]
        tail = jnp.exp(run_row_ref[h:h + 1, rows - 1:rows] - col)
        faded = (k_buf[:, cols].astype(F32) * tail).astype(BF16)
        states[me, cols, :] = dot(faded, v_buf[:, cols], ((0,), (0,))).astype(BF16)
    s_start, s_relay, s_finish, s_done = causal_ops(states, s_send, s_recv, sx_send)
    s_start()
    start_gather(OUT)
    start_gather(CROSS)

    forward(QUERY)
    finish(QUERY)
    q_buf[...] = dot(normed[...], gq[...]).astype(BF16)

    @pl.loop(0, me)
    def _(o):
        pltpu.make_async_remote_copy(
            tots.at[o], tots.at[o], t_send.at[o], t_recv.at[o],
            device_id={"seq": twin}, device_id_type=MESH).wait_recv()

    s_relay()
    s_finish()
    t_iota = lax.broadcasted_iota(jnp.int32, (rows, rows), 0)
    s_iota = lax.broadcasted_iota(jnp.int32, (rows, rows), 1)
    for h in range(heads):
        cols = slice(h * HD, (h + 1) * HD)
        col = run_col_ref[:, h:h + 1]
        causal = t_iota >= s_iota
        spread = jnp.where(causal, col - run_row_ref[h:h + 1, :], 0.0)
        decay = jnp.where(causal, jnp.exp(spread), 0.0)
        scores = dot(q_buf[:, cols], k_buf[:, cols], ((1,), (1,)))
        weighted = (scores * decay).astype(BF16)
        within = dot(weighted, v_buf[:, cols])

        def step(o, state):
            return jnp.exp(tots[o, h:h + 1, :]) * state + states[o, cols, :].astype(F32)

        incoming = lax.fori_loop(0, me, step, jnp.zeros((HD, HD), F32))
        carried = dot(
            q_buf[:, cols].astype(F32), incoming, precision=lax.Precision.HIGHEST) * jnp.exp(col)
        raw = within + carried
        ret[:, cols] = (
            raw * lax.rsqrt(jnp.mean(raw * raw, axis=-1, keepdims=True) + 1e-06)).astype(BF16)

    half = width // 2
    piece = half // 3

    def head_copy(src, dst, i, other):
        return pltpu.make_async_remote_copy(
            src, dst, h_send.at[i], h_recv.at[i], device_id={"head": other}, device_id_type=MESH)

    def project(side):
        for c in range(3):
            base = pl.multiple_of(side * half + c * piece, piece)
            term = dot(ret[...], go[pl.ds(base, piece), :], ((1,), (1,)))
            part[side, :, c * piece:(c + 1) * piece] = term.astype(BF16)

    forward(OUT)
    finish(OUT)
    project(1 - core)
    to_near = head_copy(part.at[1 - core], got_a, 0, near)
    to_near.start()
    project(core)
    to_near.wait_recv()
    pair[...] = (part[core].astype(F32) + got_a[...].astype(F32)).astype(BF16)
    to_far = head_copy(pair, got_b, 1, far)
    to_far.start()
    forward(CROSS)
    to_far.wait_recv()
    mine[...] = (pair[...].astype(F32) + got_b[...].astype(F32)).astype(BF16)
    back = head_copy(mine, got_c, 2, near)
    back.start()
    own_cols = pl.ds(pl.multiple_of(core * half, half), half)
    dec_ref[:, own_cols] = x_ref[:, own_cols].astype(F32) + mine[...].astype(F32)
    back.wait_recv()
    other_cols = pl.ds(pl.multiple_of((1 - core) * half, half), half)
    dec_ref[:, other_cols] = x_ref[:, other_cols].astype(F32) + got_c[...].astype(F32)

    @pl.loop(0, rows // 32)
    def _(i):
        part_rows = pl.ds(i * 32, 32)
        d = dec_ref[part_rows, :]
        normed[part_rows, :] = (
            d * lax.rsqrt(jnp.mean(d * d, axis=-1, keepdims=True) + 1e-06)).astype(BF16)

    finish(CROSS)
    kvs[me] = dot(normed[...], gc[:, :2 * HD]).astype(BF16)
    kv_start, kv_relay, kv_finish, kv_done = causal_ops(kvs, kv_send, kv_recv, kvx_send)
    kv_start()
    for g in range(heads):
        cols = slice((2 + g) * HD, (3 + g) * HD)
        q_rows[g * rows:(g + 1) * rows, :] = (dot(normed[...], gc[:, cols]) * HD ** -0.5).astype(BF16)

    for g in range(heads):
        block = slice(g * rows, (g + 1) * rows)
        scores = dot(q_rows[block, :], kvs[me, :, :HD], ((1,), (1,)))
        scores = jnp.where(t_iota >= s_iota, scores, -1e30)
        high = jnp.max(scores, axis=-1, keepdims=True)
        weights = jnp.exp(scores - high)
        top[block, :] = high
        total[block, :] = jnp.sum(weights, axis=-1, keepdims=True)
        acc[block, :] = dot(weights.astype(BF16), kvs[me, :, HD:])

    kv_relay()
    kv_finish()

    @pl.loop(0, me)
    def _(o):
        for g in range(heads):
            block = slice(g * rows, (g + 1) * rows)
            scores = dot(q_rows[block, :], kvs[o, :, :HD], ((1,), (1,)))
            old = top[block, :]
            high = jnp.maximum(old, jnp.max(scores, axis=-1, keepdims=True))
            weights = jnp.exp(scores - high)
            shrink = jnp.exp(old - high)
            top[block, :] = high
            total[block, :] = total[block, :] * shrink + jnp.sum(weights, axis=-1, keepdims=True)
            acc[block, :] = acc[block, :] * shrink + dot(weights.astype(BF16), kvs[o, :, HD:])

    for g in range(heads):
        block = slice(g * rows, (g + 1) * rows)
        att_ref[:, g * HD:(g + 1) * HD] = (acc[block, :] / total[block, :]).astype(BF16)

    @pl.loop(me + 1, n)
    def _(p):
        total_copy(p).wait_send()

    for m in range(5):
        finish_sends(m)
    s_done()
    kv_done()
    to_near.wait_send()
    to_far.wait_send()
    back.wait_send()


def body(n, inputs, decay_logs, wq, wk, wv, wo, kg, vg, qc):
    rows, width = inputs.shape
    inner = wq.shape[1]
    heads = inner // HD
    running = jnp.cumsum(decay_logs, axis=-1)
    run_row = jnp.pad(running, ((0, 8 - heads), (0, 0)))
    run_col = run_row.T
    totals = jnp.broadcast_to(run_row[:, -1:], (8, HD))
    wc = jnp.concatenate([kg, vg, qc], axis=1)
    vmem = pl.BlockSpec(memory_space=pltpu.VMEM)
    half = width // 2
    dma = pltpu.SemaphoreType.DMA
    half_n = n // 2
    return pl.pallas_call(
        functools.partial(kernel, n),
        out_shape=(
            jax.ShapeDtypeStruct((rows, width), F32),
            jax.ShapeDtypeStruct((rows, inner), BF16),
        ),
        in_specs=[vmem] * 9,
        out_specs=(vmem, vmem),
        scratch_shapes=[
            pltpu.VMEM((width, inner), BF16),
            pltpu.VMEM((width, inner), BF16),
            pltpu.VMEM((width, inner), BF16),
            pltpu.VMEM((width, inner), BF16),
            pltpu.VMEM((width, inner + 2 * HD), BF16),
            pltpu.VMEM((n, 8, HD), F32),
            pltpu.VMEM((n, inner, HD), BF16),
            pltpu.VMEM((n, rows, 2 * HD), BF16),
            pltpu.VMEM((rows, width), BF16),
            pltpu.VMEM((rows, inner), BF16),
            pltpu.VMEM((rows, inner), BF16),
            pltpu.VMEM((rows, inner), BF16),
            pltpu.VMEM((rows, inner), BF16),
            pltpu.VMEM((2, rows, half), BF16),
            pltpu.VMEM((rows, half), BF16),
            pltpu.VMEM((rows, half), BF16),
            pltpu.VMEM((rows, half), BF16),
            pltpu.VMEM((rows, half), BF16),
            pltpu.VMEM((rows, half), BF16),
            pltpu.VMEM((heads * rows, HD), BF16),
            pltpu.VMEM((heads * rows, 1), F32),
            pltpu.VMEM((heads * rows, 1), F32),
            pltpu.VMEM((heads * rows, HD), F32),
            dma((5, half_n)), dma((5, n)), dma((5, half_n)), dma((5,)),
            dma((n,)), dma((n,)),
            dma((half_n,)), dma((n,)), dma((half_n,)),
            dma((half_n,)), dma((n,)), dma((half_n,)),
            dma((3,)), dma((3,)),
        ],
        compiler_params=pltpu.CompilerParams(
            collective_id=0, has_side_effects=True, vmem_limit_bytes=60 * 1024 * 1024),
        name="layer",
    )(inputs, run_row, run_col, totals, wk, wv, wq, wo, wc)


def solution(mesh):
    n = mesh.shape["seq"]

    def run(*args):
        return body(n, *args)

    in_specs = (P("seq", None), P("head", "seq")) + (P("seq", "head"),) * 7
    out_specs = (P("seq", None), P("seq", "head"))
    return jax.shard_map(run, mesh=mesh, in_specs=in_specs, out_specs=out_specs, check_vma=False)
```

time: 424 us -> 230 us (0.54)
  the two profiles are of different devices: /device:TPU:0 before, /device:TPU:29 now
where the time goes in v1:
time: 230 us
  Pallas kernels  218 us (95%)
  local copies, waits for them, and re-layouts  7.75 us (3%)
  other arithmetic  2.88 us (1%)
    pallas_call x1, Pallas kernels, body(): pl.pallas_call(functools.partial(kernel, n), out_shape=(jax.ShapeDtypeStr...  218 us
    unnamed x5, local copies, waits for them, and re-layouts  4.69 us

profile of v1, /device:TPU:29, one launch (start us, length us, event | category | flops | bytes accessed | tf_op | source)
XLA Modules:
  0.0 229.6 jit_solution(514305954316104734)
XLA Ops:
  0.6 0.7 reshape.14
  1.3 0.9 reduce-window.6
  2.2 0.1 slice.12
  2.3 0.1 copy.11
  2.5 0.1 copy.12
  2.6 0.1 broadcast_add_fusion
  2.6 0.1 copy.13
  2.8 0.7 broadcast_in_dim.8.tot_ref
  3.5 0.1 copy.15
  3.5 0.7 pad_bitcast_fusion.run_col_ref
  4.2 0.6 pad.4.clone.run_row_ref
  4.8 1.9 pad_maximum_fusion.wc_ref
  6.7 218.3 %layer.1 = (f32[256,3072]{1,0:T(8,128)}, bf16[256,384]{1,0:T(8,128)(2,1)}) custom-call(bf16[256,3072]{1,0:T(8,128)(2,1)} %x_ref.1, f32[8,256]{1,0:T(8,128)} %pad.4.clone.run_row_ref, f32[256,8]{1,0:T(8,128)} %pad_bitcast_fusion.run_col_ref, f32[8,128]{1,0:T(8,128)} %broadcast_in_dim.8.tot_ref, bf16[384,384]{1,0:T(8,128)(2,1)} %wk_ref.1, ...), custom_call_target="tpu_custom_call" | custom-call | tf_op jit(solution)/shard_map/layer/pallas_call | solution.py:346
  225.0 0.0 copy-start
  225.0 3.9 %copy.18 = f32[256,3072]{1,0:T(8,128)} copy(f32[256,3072]{1,0:T(8,128)} %get-tuple-element.4) | data formatting | bytes 6291456
  228.9 0.0 copy-done
  228.9 0.7 copy.19
  (3 shorter events, 0.0 us)
Async XLA Ops:
  225.0 3.9 %copy-start = (bf16[256,384]{1,0:T(8,128)(2,1)S(1)}, bf16[256,384]{1,0:T(8,128)(2,1)}, u32[]{:S(2)}) copy-start(bf16[256,384]{1,0:T(8,128)(2,1)} %get-tuple-element.5) | copy-start | bytes 589828

commit v2 on v1

v2 whole, which is shorter than its diff:
```python
import functools

import jax
import jax.numpy as jnp
from jax import lax
from jax.experimental import pallas as pl
from jax.experimental.pallas import tpu as pltpu
from jax.sharding import PartitionSpec as P

HD = 128
F32 = jnp.float32
BF16 = jnp.bfloat16
MESH = pl.DeviceIdType.MESH
KEY, VALUE, QUERY, OUT, CROSS, KEY_GLOBAL, VALUE_GLOBAL = range(7)
PLUS = (True, False, True, False, True, False, False)


def dot(a, b, dims=((1,), (0,)), precision=None):
    return lax.dot_general(a, b, (dims, ((), ())), precision=precision, preferred_element_type=F32)


def kernel(
    n, aligned,
    x_ref, xs_ref, run_row_ref, run_col_ref, tot_ref,
    wk_ref, wv_ref, wq_ref, wo_ref, wc_ref, wkg_ref, wvg_ref,
    dec_out, att_ref,
    gk, gv, gq, go, gc, gkg, gvg, tots, states, kvs,
    dec_ref, nx, twin_nx, sent, got, within_buf,
    normed, q_buf, k_buf, v_buf, ret, part, got_a, pair, got_b, mine, got_c,
    q_rows, top, total, acc,
    wp_send, wm_send, w_recv, wx_send, w_local, t_send, t_recv,
    s_send, s_recv, sx_send, kv_send, kv_recv, kvx_send, h_send, h_recv, p_send, p_recv, out_sem,
):
    me = lax.axis_index("seq")
    head = lax.axis_index("head")
    rows, width = x_ref.shape
    heads = wq_ref.shape[1] // HD
    half_n = n // 2
    mid = half_n // 2
    odd = lax.rem(me, 2)
    twin = me + 1 - 2 * odd
    core = lax.rem(head, 2)
    near = head + 1 - 2 * core
    far = lax.rem(head + 2, 4)
    own_refs = (wk_ref, wv_ref, wq_ref, wo_ref, wc_ref, wkg_ref, wvg_ref)
    full_refs = (gk, gv, gq, go, gc, gkg, gvg)
    up = lax.rem(me + 2, n)
    down = lax.rem(me + n - 2, n)

    barrier = pltpu.get_barrier_semaphore()

    @pl.loop(0, n - 1)
    def _(k):
        pl.semaphore_signal(
            barrier, inc=1, device_id={"seq": lax.rem(me + 1 + k, n)}, device_id_type=MESH
        )

    for other in (near, far):
        pl.semaphore_signal(barrier, inc=1, device_id={"head": other}, device_id_type=MESH)
    pl.semaphore_wait(barrier, n + 1)

    def slot(m, o):
        depth = own_refs[m].shape[0]
        place = o // 2 if m < OUT else o
        return full_refs[m].at[pl.ds(pl.multiple_of(place * depth, depth), depth), :]

    def ring_copy(m, s, plus):
        o = lax.rem(me + n - 2 * s, n) if plus else lax.rem(me + 2 * s, n)
        src = own_refs[m] if s == 0 else slot(m, o)
        return pltpu.make_async_remote_copy(
            src, slot(m, o), (wp_send if plus else wm_send).at[m, s], w_recv.at[m, o],
            device_id={"seq": up if plus else down}, device_id_type=MESH)

    def x_copy(m, o, own=False):
        return pltpu.make_async_remote_copy(
            own_refs[m] if own else slot(m, o), slot(m, o), wx_send.at[m, o // 2], w_recv.at[m, o],
            device_id={"seq": twin}, device_id_type=MESH)

    def local_copy(m):
        return pltpu.make_async_copy(own_refs[m], slot(m, me), w_local.at[m])

    def start_gather(m):
        ring_copy(m, 0, True).start()
        ring_copy(m, 0, False).start()
        if m >= OUT:
            x_copy(m, me, own=True).start()
        local_copy(m).start()

    def arrive(m, o):
        x_copy(m, o).wait_recv()

    def forward(m):
        for s in range(1, mid):
            for plus in (True, False):
                o = lax.rem(me + n - 2 * s, n) if plus else lax.rem(me + 2 * s, n)
                arrive(m, o)
                if s < mid - 1 or plus == PLUS[m]:
                    ring_copy(m, s, plus).start()
                if m >= OUT:
                    x_copy(m, o).start()

    def settle(m):
        o = lax.rem(me + 2 * mid, n)
        arrive(m, o)
        if m >= OUT:
            x_copy(m, o).start()
        local_copy(m).wait()

    def finish(m):
        @pl.loop(0, half_n)
        def _(k):
            arrive(m, lax.rem(twin + 2 * k, n))

    def finish_sends(m):
        for s in range(mid):
            for plus in (True, False):
                if s < mid - 1 or plus == PLUS[m]:
                    ring_copy(m, s, plus).wait_send()
        if m >= OUT:
            x_copy(m, me, own=True).wait_send()

            @pl.loop(1, half_n)
            def _(k):
                x_copy(m, lax.rem(me + 2 * k, n)).wait_send()

    z = me // 2

    def causal_ops(buf, send, recv, x_send):
        def direct(k):
            return pltpu.make_async_remote_copy(
                buf.at[me], buf.at[me], send.at[k], recv.at[me],
                device_id={"seq": me + 2 * k}, device_id_type=MESH)

        def across(o, k):
            return pltpu.make_async_remote_copy(
                buf.at[o], buf.at[o], x_send.at[k], recv.at[o],
                device_id={"seq": twin}, device_id_type=MESH)

        def start():
            @pl.when(odd == 0)
            def _():
                across(me, 0).start()

            @pl.loop(1, half_n - z)
            def _(k):
                direct(k).start()

        def relay(use=None):
            @pl.loop(1, z + 1)
            def _(k):
                o = me - 2 * k
                across(o, k).wait_recv()
                across(o, k).start()
                if use is not None:
                    use(o)

        def finish(use=None):
            @pl.loop(0, z + odd)
            def _(k):
                across(me - 1 - 2 * k, 0).wait_recv()
                if use is not None:
                    use(me - 1 - 2 * k)

        def finish_sends():
            @pl.when(odd == 0)
            def _():
                across(me, 0).wait_send()

            @pl.loop(1, half_n - z)
            def _(k):
                direct(k).wait_send()

            @pl.loop(1, z + 1)
            def _(k):
                across(me - 2 * k, k).wait_send()

        return start, relay, finish, finish_sends

    def total_copy(p):
        return pltpu.make_async_remote_copy(
            tot_ref, tots.at[me], t_send.at[p], t_recv.at[me],
            device_id={"seq": p}, device_id_type=MESH)

    @pl.loop(me + 1, n)
    def _(p):
        total_copy(p).start()

    start_gather(KEY)
    start_gather(VALUE)
    depth = wq_ref.shape[0]

    @pl.loop(0, rows // 32)
    def _(i):
        part_rows = pl.ds(i * 32, 32)
        x = x_ref[part_rows, :].astype(F32)
        scale = lax.rsqrt(jnp.mean(x * x, axis=-1, keepdims=True) + 1e-06)
        for side in range(2):
            if aligned:
                for j in range(half_n):
                    cols = slice((2 * j + side) * depth, (2 * j + side + 1) * depth)
                    nx[side, part_rows, j * depth:(j + 1) * depth] = (
                        x_ref[part_rows, cols].astype(F32) * scale).astype(BF16)
            else:
                nx[side, part_rows, :] = (
                    xs_ref[side, part_rows, :].astype(F32) * scale).astype(BF16)

    def twin_copy(src, dst, i):
        return pltpu.make_async_remote_copy(
            src, dst, p_send.at[i], p_recv.at[i], device_id={"seq": twin}, device_id_type=MESH)

    tokens = twin_copy(nx.at[1 - odd], twin_nx, 3)
    tokens.start()

    def share(m):
        twin_part = dot(twin_nx[...], full_refs[m][...])
        sent[m] = twin_part.astype(BF16)
        twin_copy(sent.at[m], got.at[m], m).start()
        return dot(nx[odd], full_refs[m][...])

    def combine(m, own, dst):
        twin_copy(sent.at[m], got.at[m], m).wait_recv()
        dst[...] = (own + got[m].astype(F32)).astype(BF16)

    forward(KEY)
    forward(VALUE)
    start_gather(QUERY)
    tokens.wait_recv()
    settle(KEY)
    within_buf[...] = share(KEY)
    settle(VALUE)
    value_part = share(VALUE)
    combine(KEY, within_buf[...], k_buf)
    combine(VALUE, value_part, v_buf)
    forward(QUERY)
    for h in range(heads):
        cols = slice(h * HD, (h + 1) * HD)
        col = run_col_ref[:, h:h + 1]
        tail = jnp.exp(run_row_ref[h:h + 1, rows - 1:rows] - col)
        faded = (k_buf[:, cols].astype(F32) * tail).astype(BF16)
        states[me, cols, :] = dot(faded, v_buf[:, cols], ((0,), (0,))).astype(BF16)
    s_start, s_relay, s_finish, s_done = causal_ops(states, s_send, s_recv, sx_send)
    s_start()
    start_gather(OUT)
    settle(QUERY)
    query_part = share(QUERY)
    combine(QUERY, query_part, q_buf)
    t_iota = lax.broadcasted_iota(jnp.int32, (rows, rows), 0)
    s_iota = lax.broadcasted_iota(jnp.int32, (rows, rows), 1)
    for h in range(heads):
        cols = slice(h * HD, (h + 1) * HD)
        col = run_col_ref[:, h:h + 1]
        causal = t_iota >= s_iota
        spread = jnp.where(causal, col - run_row_ref[h:h + 1, :], 0.0)
        decay = jnp.where(causal, jnp.exp(spread), 0.0)
        scores = dot(q_buf[:, cols], k_buf[:, cols], ((1,), (1,)))
        weighted = (scores * decay).astype(BF16)
        within_buf[:, cols] = dot(weighted, v_buf[:, cols])

    @pl.loop(0, me)
    def _(o):
        pltpu.make_async_remote_copy(
            tots.at[o], tots.at[o], t_send.at[o], t_recv.at[o],
            device_id={"seq": twin}, device_id_type=MESH).wait_recv()

    s_relay()
    s_finish()
    for h in range(heads):
        cols = slice(h * HD, (h + 1) * HD)
        col = run_col_ref[:, h:h + 1]

        def step(o, state):
            return jnp.exp(tots[o, h:h + 1, :]) * state + states[o, cols, :].astype(F32)

        incoming = lax.fori_loop(0, me, step, jnp.zeros((HD, HD), F32))
        carried = dot(
            q_buf[:, cols].astype(F32), incoming, precision=lax.Precision.HIGHEST) * jnp.exp(col)
        raw = within_buf[:, cols] + carried
        ret[:, cols] = (
            raw * lax.rsqrt(jnp.mean(raw * raw, axis=-1, keepdims=True) + 1e-06)).astype(BF16)

    half = width // 2
    piece = half // 3

    def head_copy(src, dst, i, other):
        return pltpu.make_async_remote_copy(
            src, dst, h_send.at[i], h_recv.at[i], device_id={"head": other}, device_id_type=MESH)

    def project(side):
        for c in range(3):
            base = pl.multiple_of(side * half + c * piece, piece)
            term = dot(ret[...], go[pl.ds(base, piece), :], ((1,), (1,)))
            part[side, :, c * piece:(c + 1) * piece] = term.astype(BF16)

    forward(OUT)
    for m in (KEY_GLOBAL, VALUE_GLOBAL, CROSS):
        start_gather(m)
    settle(OUT)
    finish(OUT)
    project(1 - core)
    to_near = head_copy(part.at[1 - core], got_a, 0, near)
    to_near.start()
    project(core)
    to_near.wait_recv()
    pair[...] = (part[core].astype(F32) + got_a[...].astype(F32)).astype(BF16)
    to_far = head_copy(pair, got_b, 1, far)
    to_far.start()
    for m in (KEY_GLOBAL, VALUE_GLOBAL, CROSS):
        forward(m)
    to_far.wait_recv()
    mine[...] = (pair[...].astype(F32) + got_b[...].astype(F32)).astype(BF16)
    back = head_copy(mine, got_c, 2, near)
    back.start()
    for m in (KEY_GLOBAL, VALUE_GLOBAL, CROSS):
        settle(m)
    own_cols = pl.ds(pl.multiple_of(core * half, half), half)
    dec_ref[:, own_cols] = x_ref[:, own_cols].astype(F32) + mine[...].astype(F32)
    back.wait_recv()
    other_cols = pl.ds(pl.multiple_of((1 - core) * half, half), half)
    dec_ref[:, other_cols] = x_ref[:, other_cols].astype(F32) + got_c[...].astype(F32)

    @pl.loop(0, rows // 32)
    def _(i):
        part_rows = pl.ds(i * 32, 32)
        d = dec_ref[part_rows, :]
        normed[part_rows, :] = (
            d * lax.rsqrt(jnp.mean(d * d, axis=-1, keepdims=True) + 1e-06)).astype(BF16)

    dec_copy = pltpu.make_async_copy(dec_ref, dec_out, out_sem)
    dec_copy.start()
    finish(KEY_GLOBAL)
    finish(VALUE_GLOBAL)
    kvs[me, :, :HD] = dot(normed[...], gkg[...]).astype(BF16)
    kvs[me, :, HD:] = dot(normed[...], gvg[...]).astype(BF16)
    kv_start, kv_relay, kv_finish, kv_done = causal_ops(kvs, kv_send, kv_recv, kvx_send)
    kv_start()
    finish(CROSS)
    cross = (dot(normed[...], gc[...]) * HD ** -0.5).astype(BF16)
    for g in range(heads):
        q_rows[g * rows:(g + 1) * rows, :] = cross[:, g * HD:(g + 1) * HD]

    for g in range(heads):
        block = slice(g * rows, (g + 1) * rows)
        scores = dot(q_rows[block, :], kvs[me, :, :HD], ((1,), (1,)))
        scores = jnp.where(t_iota >= s_iota, scores, -1e30)
        high = jnp.max(scores, axis=-1, keepdims=True)
        weights = jnp.exp(scores - high)
        top[block, :] = high
        total[block, :] = jnp.sum(weights, axis=-1, keepdims=True)
        acc[block, :] = dot(weights.astype(BF16), kvs[me, :, HD:])

    def attend(o):
        for g in range(heads):
            block = slice(g * rows, (g + 1) * rows)
            scores = dot(q_rows[block, :], kvs[o, :, :HD], ((1,), (1,)))
            old = top[block, :]
            high = jnp.maximum(old, jnp.max(scores, axis=-1, keepdims=True))
            weights = jnp.exp(scores - high)
            shrink = jnp.exp(old - high)
            top[block, :] = high
            total[block, :] = total[block, :] * shrink + jnp.sum(weights, axis=-1, keepdims=True)
            acc[block, :] = acc[block, :] * shrink + dot(weights.astype(BF16), kvs[o, :, HD:])

    kv_relay(attend)
    kv_finish(attend)

    for g in range(heads):
        block = slice(g * rows, (g + 1) * rows)
        att_ref[:, g * HD:(g + 1) * HD] = (acc[block, :] / total[block, :]).astype(BF16)

    @pl.loop(me + 1, n)
    def _(p):
        total_copy(p).wait_send()

    for m in range(7):
        finish_sends(m)
    tokens.wait_send()
    for m in range(3):
        twin_copy(sent.at[m], got.at[m], m).wait_send()
    dec_copy.wait()
    s_done()
    kv_done()
    to_near.wait_send()
    to_far.wait_send()
    back.wait_send()


def body(n, inputs, decay_logs, wq, wk, wv, wo, kg, vg, qc):
    rows, width = inputs.shape
    inner = wq.shape[1]
    heads = inner // HD
    running = jnp.cumsum(decay_logs, axis=-1)
    run_row = jnp.pad(running, ((0, 8 - heads), (0, 0)))
    run_col = run_row.T
    totals = jnp.broadcast_to(run_row[:, -1:], (8, HD))
    depth = wq.shape[0]
    aligned = depth % HD == 0
    half_n = n // 2
    half = width // 2
    small = inputs[:16, :HD].reshape(1, 16, HD)
    split = inputs.reshape(rows, half_n, 2, depth).transpose(2, 0, 1, 3).reshape(2, rows, half)
    vmem = pl.BlockSpec(memory_space=pltpu.VMEM)
    dma = pltpu.SemaphoreType.DMA
    mid = max(half_n // 2, 1)
    return pl.pallas_call(
        functools.partial(kernel, n, aligned),
        out_shape=(
            jax.ShapeDtypeStruct((rows, width), F32),
            jax.ShapeDtypeStruct((rows, inner), BF16),
        ),
        in_specs=[vmem] * 12,
        out_specs=(pl.BlockSpec(memory_space=pl.ANY), vmem),
        scratch_shapes=[
            pltpu.VMEM((half, inner), BF16),
            pltpu.VMEM((half, inner), BF16),
            pltpu.VMEM((half, inner), BF16),
            pltpu.VMEM((width, inner), BF16),
            pltpu.VMEM((width, inner), BF16),
            pltpu.VMEM((width, HD), BF16),
            pltpu.VMEM((width, HD), BF16),
            pltpu.VMEM((n, 8, HD), F32),
            pltpu.VMEM((n, inner, HD), BF16),
            pltpu.VMEM((n, rows, 2 * HD), BF16),
            pltpu.VMEM((rows, width), F32),
            pltpu.VMEM((2, rows, half), BF16),
            pltpu.VMEM((rows, half), BF16),
            pltpu.VMEM((3, rows, inner), BF16),
            pltpu.VMEM((3, rows, inner), BF16),
            pltpu.VMEM((rows, inner), F32),
            pltpu.VMEM((rows, width), BF16),
            pltpu.VMEM((rows, inner), BF16),
            pltpu.VMEM((rows, inner), BF16),
            pltpu.VMEM((rows, inner), BF16),
            pltpu.VMEM((rows, inner), BF16),
            pltpu.VMEM((2, rows, half), BF16),
            pltpu.VMEM((rows, half), BF16),
            pltpu.VMEM((rows, half), BF16),
            pltpu.VMEM((rows, half), BF16),
            pltpu.VMEM((rows, half), BF16),
            pltpu.VMEM((rows, half), BF16),
            pltpu.VMEM((heads * rows, HD), BF16),
            pltpu.VMEM((heads * rows, 1), F32),
            pltpu.VMEM((heads * rows, 1), F32),
            pltpu.VMEM((heads * rows, HD), F32),
            dma((7, mid)), dma((7, mid)), dma((7, n)), dma((7, half_n)), dma((7,)),
            dma((n,)), dma((n,)),
            dma((half_n,)), dma((n,)), dma((half_n,)),
            dma((half_n,)), dma((n,)), dma((half_n,)),
            dma((3,)), dma((3,)), dma((4,)), dma((4,)), dma,
        ],
        compiler_params=pltpu.CompilerParams(
            collective_id=0, has_side_effects=True, vmem_limit_bytes=62 * 1024 * 1024),
        name="layer",
    )(inputs, small if aligned else split, run_row, run_col, totals, wk, wv, wq, wo, qc, kg, vg)


def solution(mesh):
    n = mesh.shape["seq"]

    def run(*args):
        return body(n, *args)

    in_specs = (P("seq", None), P("head", "seq")) + (P("seq", "head"),) * 7
    out_specs = (P("seq", None), P("seq", "head"))
    return jax.shard_map(run, mesh=mesh, in_specs=in_specs, out_specs=out_specs, check_vma=False)
```

time: 230 us -> 183 us (0.80)
  Pallas kernels: 218 us -> 171 us
    pallas_call x1, Pallas kernels: 218 us -> 171 us  [body(): pl.pallas_call(functools.partial(kernel, n, aligned), out_shape=(jax.Shap...]
where the time goes in v2:
time: 183 us; the launch traced here: 182 us
  Pallas kernels  171 us (93%)
  local copies, waits for them, and re-layouts  9.03 us (5%)
    pallas_call x1, Pallas kernels, body(): pl.pallas_call(functools.partial(kernel, n, aligned), out_shape=(jax.Shap...  171 us
    unnamed x5, local copies, waits for them, and re-layouts  4.69 us

profile of v2, /device:TPU:29, one launch (start us, length us, event | category | flops | bytes accessed | tf_op | source)
XLA Modules:
  0.0 182.0 jit_solution(11395909975141326706)
XLA Ops:
  0.6 0.7 reshape.18
  1.3 0.9 reduce-window.6
  2.2 0.1 slice.16
  2.3 0.1 copy.11
  2.5 0.1 copy.12
  2.6 0.1 broadcast_add_fusion
  2.6 1.3 slice_bitcast_fusion.xs_ref
  3.9 0.1 copy.13
  4.1 0.7 broadcast_in_dim.8.tot_ref
  4.7 0.1 copy.15
  4.8 0.7 pad_bitcast_fusion.run_col_ref
  5.5 0.6 pad.4.clone.run_row_ref
  6.1 171.3 %layer.1 = (f32[256,3072]{1,0:T(8,128)}, bf16[256,384]{1,0:T(8,128)(2,1)}) custom-call(bf16[256,3072]{1,0:T(8,128)(2,1)} %x_ref.1, bf16[1,16,128]{2,1,0:T(8,128)(2,1)} %slice_bitcast_fusion.xs_ref, f32[8,256]{1,0:T(8,128)} %pad.4.clone.run_row_ref, f32[256,8]{1,0:T(8,128)} %pad_bitcast_fusion.run_col_ref, f32[8,128]{1,0:T(8,128)} %broadcast_in_dim.8.tot_ref, ...), custom_call_target="tpu_custom_call" | custom-call | tf_op jit(solution)/shard_map/layer/pallas_call | solution.py:404
  177.4 0.0 copy-start
  177.4 3.9 %copy.18 = f32[256,3072]{1,0:T(8,128)} copy(f32[256,3072]{1,0:T(8,128)} %get-tuple-element.4) | data formatting | bytes 6291456
  181.3 0.0 copy-done
  181.3 0.7 copy.19
  (3 shorter events, 0.0 us)
Async XLA Ops:
  177.4 3.9 %copy-start = (bf16[256,384]{1,0:T(8,128)(2,1)S(1)}, bf16[256,384]{1,0:T(8,128)(2,1)}, u32[]{:S(2)}) copy-start(bf16[256,384]{1,0:T(8,128)(2,1)} %get-tuple-element.5) | copy-start | bytes 589828
